TPU v7x, 32 devices: a whole 2x2x4 slice. The times are simulated.
32 devices in a mesh: owner: 8 (over y, x, core), rows: 4 (over z).
Axes of the slice: x: 2, y: 2, z: 4, core: 2. Of those that a mesh axis runs over, the one named last changes fastest.
Arguments:
- w_down: float32 [64, 1024, 2048], P('owner', None, 'rows'), may hold values from -0.1875 to 0.1875
- router_weight: float32 [2048, 64], P('rows', 'owner'), may hold values from -0.125 to 0.125
- router_gain: float32 [2048], P('rows'), may hold values from 0.25 to 1.75
Outputs:
- serve_down: bfloat16 [64, 2048, 1024], P('owner')
- serve_router: bfloat16 [2048, 64], replicated
All inputs are finite; a program needn't handle non-finite values.
Results may differ from a plain program's by a relative error of at most 0.001.
Values may be sent and summed in bfloat16 or wider, within the bound.
A program may use at most 128 MiB of HBM per device.

v0:
```python
import jax
import jax.numpy as jnp
from jax import lax
from jax.sharding import PartitionSpec as P


def shards(w_down, router_weight, router_gain):
    narrow_down = w_down.astype(jnp.bfloat16)
    serve_down = lax.all_gather(narrow_down, "rows", axis=2, tiled=True)
    serve_down = jnp.transpose(serve_down, (0, 2, 1))
    part_router = (router_weight * router_gain[:, None]).astype(jnp.bfloat16)
    row_router = lax.all_gather(part_router, "rows", axis=0, tiled=True)
    serve_router = lax.all_gather(row_router, "owner", axis=1, tiled=True)
    return (serve_down, serve_router)


def solution(mesh):
    in_specs = (P("owner", None, "rows"), P("rows", "owner"), P("rows"))
    out_specs = (P("owner", None, None), P())
    return jax.shard_map(shards, mesh=mesh, in_specs=in_specs, out_specs=out_specs, check_vma=False)
```

profile of v0, /device:TPU:0, one launch (start us, length us, event | category | flops | bytes accessed | tf_op | source)
XLA Modules:
  0.0 615.9 jit_solution(6089209621411756597)
XLA Ops:
  7.2 0.0 copy-start
  7.2 0.0 copy-start.1
  7.2 0.0 all-gather.2.cloned.1.call-start
  7.2 13.6 %copy.5 = bf16[8,1024,512]{1,2,0:T(8,128)(2,1)} copy(f32[8,1024,512]{2,1,0:T(8,128)} %param.3) | data formatting | bytes 25165824 | tf_op args[0]
  20.8 0.0 all-gather.2.cloned.1.call-update
  20.8 0.0 copy-done
  20.8 0.0 copy-done.1
  20.9 14.8 %all_gather.10 = bf16[2048,8]{0,1:T(8,128)(2,1)S(1)} all-gather(bf16[512,8]{0,1:T(8,128)(2,1)S(1)} %multiply_convert_fusion), channel_id=1, replica_groups=mesh['owner'=8,'rows'=4] {'rows'}, dimensions={0}, use_global_device_ids=true | all-gather | bytes 40960 | tf_op jit(solution)/shard_map/all_gather | solution.py:12
  35.7 9.3 %all_gather.11 = bf16[2048,64]{0,1:T(8,128)(2,1)S(1)} all-gather(bf16[2048,8]{0,1:T(8,128)(2,1)S(1)} %all_gather.10), channel_id=1, replica_groups=mesh['owner'=8,'rows'=4] {'owner'}, dimensions={1}, use_global_device_ids=true | all-gather | bytes 294912 | tf_op jit(solution)/shard_map/all_gather | solution.py:13
  45.0 540.1 %all-gather.2.cloned.1.call-done = bf16[8,1024,2048]{1,2,0:T(8,128)(2,1)} async-done(((bf16[8,1024,512]{1,2,0:T(8,128)(2,1)}), bf16[8,1024,2048]{1,2,0:T(8,128)(2,1)}) %all-gather.2.cloned.1.call-update) | async-done | bytes 33554448 | tf_op jit(solution)/shard_map/all_gather | solution.py:9
  585.1 23.2 %copy.8 = bf16[8,2048,1024]{2,1,0:T(8,128)(2,1)} copy(bf16[8,2048,1024]{2,1,0:T(8,128)(2,1)} %bitcast.1) | data formatting | bytes 67108864
  608.3 0.7 copy.9
  (1 shorter events, 0.0 us)
Async XLA Ops:
  7.2 13.7 %copy-start = (f32[512,8]{0,1:T(8,128)S(1)}, f32[512,8]{0,1:T(8,128)}, u32[]{:S(2)}) copy-start(f32[512,8]{0,1:T(8,128)} %param.4) | copy-start | bytes 49156
  7.2 13.7 %copy-start.1 = (f32[512]{0:T(512)S(1)}, f32[512]{0:T(512)}, u32[]{:S(2)}) copy-start(f32[512]{0:T(512)} %param.5) | copy-start | bytes 6148
  7.2 577.9 %all-gather.2.cloned.1.call-start = ((), (), s32[]{:S(2)}) async-start(), calls=%async_computation | async-start | bytes 41943040 | tf_op jit(solution)/shard_map/all_gather | solution.py:9
Sparse Core Ops, SparseCore 0:
  20.9 564.0 all-gather.1
where the time goes:
time: 616 us
  waiting for transfers between devices  540 us (88%)
  local copies, waits for them, and re-layouts  37.5 us (6%)
  blocking collectives  24.1 us (4%)
  between operations  14.1 us (2%)
    all_gather x1, waiting for transfers between devices, shards(): serve_down = lax.all_gather(narrow_down, 'rows', axis=2, tiled=True)  540 us
    unnamed x7, local copies, waits for them, and re-layouts  37.5 us
    all_gather x1, blocking collectives, shards(): row_router = lax.all_gather(part_router, 'rows', axis=0, tiled=True)  14.8 us
  transfers between devices with their start and end apart: 1, of which 1 were waited for; matrix products, arithmetic and copies ran while one was open for 0% of the time, Pallas kernels for 0%

commit v1 on v0

v1 whole, which is shorter than its diff:
```python
import functools

import jax
import jax.numpy as jnp
from jax import lax
from jax.experimental import pallas as pl
from jax.experimental.pallas import tpu as pltpu
from jax.sharding import PartitionSpec as P

MESH = pl.DeviceIdType.MESH
TAIL = 1


def gather_kernel(n, owners, tail, w_ref, part_ref, down_ref, router_ref, wide, own, load_sem, local_sem,
                  send_sem, recv_sem, router_local, rows_send, rows_recv, owner_send, owner_recv):
    me = lax.axis_index("rows")
    mine = lax.axis_index("owner")
    experts, depth, width = w_ref.shape
    last = n - 1

    def rows_of(block):
        return pl.ds(pl.multiple_of(block * width, width), width)

    barrier = pltpu.get_barrier_semaphore()

    @pl.loop(1, n)
    def _(d):
        pl.semaphore_signal(barrier, inc=1, device_id={"rows": lax.rem(me + d, n)}, device_id_type=MESH)

    @pl.loop(1, owners)
    def _(d):
        pl.semaphore_signal(barrier, inc=1, device_id={"owner": lax.rem(mine + d, owners)}, device_id_type=MESH)

    def load(e, slot):
        return pltpu.make_async_copy(w_ref.at[e], wide.at[slot], load_sem.at[slot])

    def keep(e):
        return pltpu.make_async_copy(own.at[e], down_ref.at[e, rows_of(me), :], local_sem.at[e])

    def send(src, way, hop, e, block):
        peer = me + 1 if way == 0 else me - 1
        return pltpu.make_async_remote_copy(
            src_ref=src, dst_ref=down_ref.at[e, rows_of(block), :],
            send_sem=send_sem.at[way, hop, e], recv_sem=recv_sem.at[way, hop, e],
            device_id={"rows": peer}, device_id_type=MESH)

    def rows_copy(peer):
        return pltpu.make_async_remote_copy(
            src_ref=part_ref, dst_ref=router_ref.at[mine, me],
            send_sem=rows_send.at[peer], recv_sem=rows_recv.at[me],
            device_id={"rows": peer}, device_id_type=MESH)

    def rows_arrival(peer):
        return pltpu.make_async_remote_copy(
            src_ref=part_ref, dst_ref=router_ref.at[mine, peer],
            send_sem=rows_send.at[peer], recv_sem=rows_recv.at[peer],
            device_id={"rows": peer}, device_id_type=MESH)

    def owner_copy(peer):
        return pltpu.make_async_remote_copy(
            src_ref=router_ref.at[mine], dst_ref=router_ref.at[mine],
            send_sem=owner_send.at[peer], recv_sem=owner_recv.at[mine],
            device_id={"owner": peer}, device_id_type=MESH)

    def owner_arrival(peer):
        return pltpu.make_async_remote_copy(
            src_ref=router_ref.at[mine], dst_ref=router_ref.at[peer],
            send_sem=owner_send.at[peer], recv_sem=owner_recv.at[peer],
            device_id={"owner": peer}, device_id_type=MESH)

    load(0, 0).start()
    own_part = pltpu.make_async_copy(part_ref, router_ref.at[mine, me], router_local)
    own_part.start()

    @pl.loop(0, experts)
    def _(e):
        slot = lax.rem(e, 2)

        @pl.when(e + 1 < experts)
        def _():
            load(e + 1, 1 - slot).start()

        load(e, slot).wait()
        own[e] = wide[slot].astype(jnp.bfloat16).T

        @pl.when(e == 0)
        def _():
            pl.semaphore_wait(barrier, n - 1 + owners - 1)

            @pl.loop(1, n)
            def _(d):
                rows_copy(lax.rem(me + d, n)).start()

        @pl.when(me < last)
        def _():
            send(own.at[e], 0, 0, e, me).start()

        @pl.when(me > 0)
        def _():
            send(own.at[e], 1, 0, e, me).start()

        keep(e).start()

    own_part.wait()

    @pl.loop(1, n)
    def _(d):
        rows_arrival(lax.rem(me + d, n)).wait_recv()

    @pl.loop(1, owners)
    def _(d):
        owner_copy(lax.rem(mine + d, owners)).start()

    def pass_on(k):
        hop = k // experts
        e = lax.rem(k, experts)
        ahead = me - 1 - hop
        behind = me + 1 + hop

        @pl.when(ahead >= 0)
        def _():
            block = down_ref.at[e, rows_of(ahead), :]
            send(block, 0, hop, e, ahead).wait_recv()
            on = (me < last) & ((hop + 2 < last) | (e < experts - tail))

            @pl.when(on)
            def _():
                send(block, 0, hop + 1, e, ahead).start()

        @pl.when(behind < n)
        def _():
            block = down_ref.at[e, rows_of(behind), :]
            send(block, 1, hop, e, behind).wait_recv()
            on = (me > 0) & ((hop + 2 < last) | (e < experts - tail))

            @pl.when(on)
            def _():
                send(block, 1, hop + 1, e, behind).start()

    @pl.loop(0, last * experts - tail)
    def _(k):
        pass_on(k)

    @pl.loop(0, experts)
    def _(e):
        keep(e).wait()

    @pl.loop(0, last * experts - tail)
    def _(k):
        hop = k // experts
        e = lax.rem(k, experts)
        ahead = me - hop
        behind = me + hop

        @pl.when((ahead >= 0) & (me < last))
        def _():
            send(own.at[e], 0, hop, e, me).wait_send()

        @pl.when((behind < n) & (me > 0))
        def _():
            send(own.at[e], 1, hop, e, me).wait_send()

    @pl.loop(1, n)
    def _(d):
        rows_copy(lax.rem(me + d, n)).wait_send()

    @pl.loop(1, owners)
    def _(d):
        owner_arrival(lax.rem(mine + d, owners)).wait_recv()
        owner_copy(lax.rem(mine + d, owners)).wait_send()


def copy_kernel(src_ref, dst_ref):
    dst_ref[...] = src_ref[...]


def place_kernel(n, tail, down_ref, piece_ref, out_ref, sem):
    me = lax.axis_index("rows")
    experts = out_ref.shape[0]
    width = piece_ref.shape[1]

    def place(block):
        return pltpu.make_async_copy(
            piece_ref, out_ref.at[pl.ds(experts - tail, tail), pl.ds(block * width, width), :], sem)

    @pl.when(me == 0)
    def _():
        place(n - 1).start()
        place(n - 1).wait()

    @pl.when(me == n - 1)
    def _():
        place(0).start()
        place(0).wait()


def shards(n, owners, w_down, router_weight, router_gain):
    experts, depth, width = w_down.shape
    tail = TAIL if n > 2 else 0
    part = (router_weight * router_gain[:, None]).astype(jnp.bfloat16).T
    cols, rows = part.shape
    hbm = pl.BlockSpec(memory_space=pl.ANY)
    vmem = pl.BlockSpec(memory_space=pltpu.VMEM)
    down, router = pl.pallas_call(
        functools.partial(gather_kernel, n, owners, tail),
        out_shape=(jax.ShapeDtypeStruct((experts, n * width, depth), jnp.bfloat16),
                   jax.ShapeDtypeStruct((owners, n, cols, rows), jnp.bfloat16)),
        in_specs=[hbm, vmem],
        out_specs=(hbm, vmem),
        scratch_shapes=[
            pltpu.VMEM((2, depth, width), jnp.float32),
            pltpu.VMEM((experts, width, depth), jnp.bfloat16),
            pltpu.SemaphoreType.DMA((2,)),
            pltpu.SemaphoreType.DMA((experts,)),
            pltpu.SemaphoreType.DMA((2, n - 1, experts)),
            pltpu.SemaphoreType.DMA((2, n - 1, experts)),
            pltpu.SemaphoreType.DMA,
            pltpu.SemaphoreType.DMA((n,)),
            pltpu.SemaphoreType.DMA((n,)),
            pltpu.SemaphoreType.DMA((owners,)),
            pltpu.SemaphoreType.DMA((owners,)),
        ],
        compiler_params=pltpu.CompilerParams(collective_id=0, has_side_effects=True,
                                             vmem_limit_bytes=40 * 1024 * 1024),
    )(w_down, part)
    serve_router = router.transpose(1, 3, 0, 2).reshape(n * rows, owners * cols)
    if tail == 0:
        return down, serve_router
    me = lax.axis_index("rows")
    start = jnp.where(me == n - 2, 0, (n - 1) * width)
    piece = lax.dynamic_slice(down, (experts - tail, start, 0), (tail, width, depth))
    piece = lax.ppermute(piece, "rows", [(n - 2, n - 1), (1, 0)])
    block = (1, n * width // 2, depth)
    out = pl.pallas_call(
        copy_kernel,
        out_shape=jax.ShapeDtypeStruct(down.shape, down.dtype),
        grid=(experts, 2),
        in_specs=[pl.BlockSpec(block, lambda e, h: (e, h, 0))],
        out_specs=pl.BlockSpec(block, lambda e, h: (e, h, 0)),
        cost_estimate=pl.CostEstimate(flops=0, transcendentals=0, bytes_accessed=4 * down.size),
    )(down)
    out = pl.pallas_call(
        functools.partial(place_kernel, n, tail),
        out_shape=jax.ShapeDtypeStruct(down.shape, down.dtype),
        in_specs=[hbm, vmem],
        out_specs=hbm,
        scratch_shapes=[pltpu.SemaphoreType.DMA],
        input_output_aliases={0: 0},
    )(out, piece)
    return out, serve_router


def solution(mesh):
    n, owners = mesh.shape["rows"], mesh.shape["owner"]
    in_specs = (P("owner", None, "rows"), P("rows", "owner"), P("rows"))
    out_specs = (P("owner", None, None), P())
    return jax.shard_map(functools.partial(shards, n, owners), mesh=mesh, in_specs=in_specs,
                         out_specs=out_specs, check_vma=False)
```

time: 616 us -> 561 us (0.911)
  Pallas kernels: 0 us -> 555 us
  waiting for transfers between devices: 540 us -> 0.01 us
  local copies, waits for them, and re-layouts: 37.5 us -> 2.98 us
  blocking collectives: 24.1 us -> 0 us
  between operations: 14.1 us -> 0.67 us
    pallas_call x0 -> x3, Pallas kernels: none -> 555 us  [the longest x1 526 us: shards(): pl.pallas_call(functools.partial(gather_kernel, n, owners, tail), out_sha...]
    all_gather x1 -> x0, waiting for transfers between devices: 540 us -> none  [shards(): serve_down = lax.all_gather(narrow_down, 'rows', axis=2, tiled=True)]
    unnamed x7 -> x3, local copies, waits for them, and re-layouts: 37.5 us -> 1.68 us
    all_gather x2 -> x0, blocking collectives: 24.1 us -> none  [the longest x1 14.8 us: shards(): row_router = lax.all_gather(part_router, 'rows', axis=0, tiled=True)]
  transfers between devices with their start and end apart: 1 -> 1, of which waited for: 1 -> 0; matrix products, arithmetic and copies ran while one was open for 0% -> 0% of each run, Pallas kernels for 0% -> 5%
where the time goes in v1:
time: 561 us
  Pallas kernels  555 us (99%)
    pallas_call x1, Pallas kernels, shards(): pl.pallas_call(functools.partial(gather_kernel, n, owners, tail), out_sha...  526 us
    pallas_call x1, Pallas kernels, shards(): pl.pallas_call(copy_kernel, out_shape=jax.ShapeDtypeStruct(down.shape, do...  27.2 us
  transfers between devices with their start and end apart: 1, of which 0 were waited for; matrix products, arithmetic and copies ran while one was open for 0% of the time, Pallas kernels for 5%

profile of v1, /device:TPU:0, one launch (start us, length us, event | category | flops | bytes accessed | tf_op | source)
XLA Modules:
  0.0 560.6 jit_solution(7460988382732955894)
XLA Ops:
  0.6 0.7 fusion.part_ref
  1.4 525.6 %shard_map.50 = (bf16[8,2048,1024]{2,1,0:T(8,128)(2,1)}, bf16[8,4,8,512]{3,2,1,0:T(8,128)(2,1)S(1)}) custom-call(f32[8,1024,512]{2,1,0:T(8,128)} %w_ref.1, bf16[8,512]{1,0:T(8,128)(2,1)S(1)} %fusion.part_ref), custom_call_target="tpu_custom_call" | custom-call | tf_op jit(solution)/shard_map/pallas_call | solution.py:204
  526.9 1.3 constant_dynamic-slice_fusion
  528.2 1.3 collective-permute-start
  529.5 27.2 %shard_map.51.down_ref = bf16[8,2048,1024]{2,1,0:T(8,128)(2,1)} custom-call(bf16[8,2048,1024]{2,1,0:T(8,128)(2,1)} %get-tuple-element.4.src_ref), custom_call_target="tpu_custom_call" | custom-call | bytes 67108864 | tf_op jit(solution)/shard_map/pallas_call | solution.py:234
  556.7 0.0 collective-permute-done.piece_ref
  556.8 0.0 copy-start
  556.8 1.0 copy-done
  557.7 2.2 shard_map.52
  559.9 0.7 copy.8
Async XLA Ops:
  528.2 28.5 %collective-permute-start = (bf16[1,512,1024]{2,1,0:T(8,128)(2,1)S(1)}, bf16[1,512,1024]{2,1,0:T(8,128)(2,1)S(1)}, u32[]{:S(2)}, u32[]{:S(2)}) collective-permute-start(bf16[1,512,1024]{2,1,0:T(8,128)(2,1)S(1)} %constant_dynamic-slice_fusion), channel_id=1, source_target_pairs={{2,3},{1,0},{6,7},{5,4},{10,11},{9,8},{14,15},{13,12},{18,19},{17,... | collective-permute-start | bytes 3145736 | tf_op jit(solution)/shard_map/ppermute | solution.py:232
  556.8 1.0 copy-start

commit v2 on v1

--- a/solution.py
+++ b/solution.py
@@ -8,7 +8,7 @@
 from jax.sharding import PartitionSpec as P
 
 MESH = pl.DeviceIdType.MESH
-TAIL = 1
+TAIL = 2
 
 
 def gather_kernel(n, owners, tail, w_ref, part_ref, down_ref, router_ref, wide, own, load_sem, local_sem,
@@ -174,14 +174,13 @@
     dst_ref[...] = src_ref[...]
 
 
-def place_kernel(n, tail, down_ref, piece_ref, out_ref, sem):
+def place_kernel(n, expert, down_ref, piece_ref, out_ref, sem):
     me = lax.axis_index("rows")
-    experts = out_ref.shape[0]
     width = piece_ref.shape[1]
 
     def place(block):
         return pltpu.make_async_copy(
-            piece_ref, out_ref.at[pl.ds(experts - tail, tail), pl.ds(block * width, width), :], sem)
+            piece_ref, out_ref.at[pl.ds(expert, 1), pl.ds(block * width, width), :], sem)
 
     @pl.when(me == 0)
     def _():
@@ -196,7 +195,7 @@
 
 def shards(n, owners, w_down, router_weight, router_gain):
     experts, depth, width = w_down.shape
-    tail = TAIL if n > 2 else 0
+    tail = min(TAIL, experts) if n > 3 else 0
     part = (router_weight * router_gain[:, None]).astype(jnp.bfloat16).T
     cols, rows = part.shape
     hbm = pl.BlockSpec(memory_space=pl.ANY)
@@ -228,8 +227,11 @@
         return down, serve_router
     me = lax.axis_index("rows")
     start = jnp.where(me == n - 2, 0, (n - 1) * width)
-    piece = lax.dynamic_slice(down, (experts - tail, start, 0), (tail, width, depth))
-    piece = lax.ppermute(piece, "rows", [(n - 2, n - 1), (1, 0)])
+    late = range(experts - tail, experts)
+    pieces = []
+    for e in late:
+        piece = lax.dynamic_slice(down, (e, start, 0), (1, width, depth))
+        pieces.append(lax.ppermute(piece, "rows", [(n - 2, n - 1), (1, 0)]))
     block = (1, n * width // 2, depth)
     out = pl.pallas_call(
         copy_kernel,
@@ -237,16 +239,20 @@
         grid=(experts, 2),
         in_specs=[pl.BlockSpec(block, lambda e, h: (e, h, 0))],
         out_specs=pl.BlockSpec(block, lambda e, h: (e, h, 0)),
+        compiler_params=pltpu.CompilerParams(vmem_limit_bytes=24 * 1024 * 1024),
         cost_estimate=pl.CostEstimate(flops=0, transcendentals=0, bytes_accessed=4 * down.size),
     )(down)
-    out = pl.pallas_call(
-        functools.partial(place_kernel, n, tail),
-        out_shape=jax.ShapeDtypeStruct(down.shape, down.dtype),
-        in_specs=[hbm, vmem],
-        out_specs=hbm,
-        scratch_shapes=[pltpu.SemaphoreType.DMA],
-        input_output_aliases={0: 0},
-    )(out, piece)
+    for e, piece in zip(late, pieces):
+        out = pl.pallas_call(
+            functools.partial(place_kernel, n, e),
+            out_shape=jax.ShapeDtypeStruct(down.shape, down.dtype),
+            in_specs=[hbm, vmem],
+            out_specs=hbm,
+            scratch_shapes=[pltpu.SemaphoreType.DMA],
+            input_output_aliases={0: 0},
+            compiler_params=pltpu.CompilerParams(vmem_limit_bytes=8 * 1024 * 1024),
+            cost_estimate=pl.CostEstimate(flops=0, transcendentals=0, bytes_accessed=4 * piece.size),
+        )(out, piece)
     return out, serve_router
 
 

time: 561 us -> 557 us (level)
  Pallas kernels: 555 us -> 532 us
  waiting for transfers between devices: 0.01 us -> 18 us
    pallas_call x1, Pallas kernels: 526 us -> 503 us  [shards(): pl.pallas_call(functools.partial(gather_kernel, n, owners, tail), out_sha...]
    ppermute x1 -> x2, waiting for transfers between devices: 0.01 us -> 18 us  [shards(): pieces.append(lax.ppermute(piece, 'rows', [(n - 2, n - 1), (1, 0)]))]
  transfers between devices with their start and end apart: 1 -> 2, of which waited for: 0 -> 1; matrix products, arithmetic and copies ran while one was open for 0% -> 0% of each run, Pallas kernels for 5% -> 5%
where the time goes in v2:
time: 557 us
  Pallas kernels  532 us (96%)
  waiting for transfers between devices  18 us (3%)
    pallas_call x1, Pallas kernels, shards(): pl.pallas_call(functools.partial(gather_kernel, n, owners, tail), out_sha...  503 us
    pallas_call x1, Pallas kernels, shards(): pl.pallas_call(copy_kernel, out_shape=jax.ShapeDtypeStruct(down.shape, do...  27.2 us
    ppermute x2, waiting for transfers between devices, shards(): pieces.append(lax.ppermute(piece, 'rows', [(n - 2, n - 1), (1, 0)]))  18 us
  transfers between devices with their start and end apart: 2, of which 1 were waited for; matrix products, arithmetic and copies ran while one was open for 0% of the time, Pallas kernels for 5%

profile of v2, /device:TPU:0, one launch (start us, length us, event | category | flops | bytes accessed | tf_op | source)
XLA Modules:
  0.0 556.7 jit_solution(2812190251286261495)
XLA Ops:
  0.6 0.7 fusion.part_ref
  1.4 503.1 %shard_map.50 = (bf16[8,2048,1024]{2,1,0:T(8,128)(2,1)}, bf16[8,4,8,512]{3,2,1,0:T(8,128)(2,1)S(1)}) custom-call(f32[8,1024,512]{2,1,0:T(8,128)} %w_ref.1, bf16[8,512]{1,0:T(8,128)(2,1)S(1)} %fusion.part_ref), custom_call_target="tpu_custom_call" | custom-call | tf_op jit(solution)/shard_map/pallas_call | solution.py:203
  504.4 1.7 constant_dynamic-slice_fusion
  506.2 1.3 collective-permute-start
  507.5 1.3 collective-permute-start.1
  508.8 27.2 %shard_map.51.down_ref = bf16[8,2048,1024]{2,1,0:T(8,128)(2,1)} custom-call(bf16[8,2048,1024]{2,1,0:T(8,128)(2,1)} %get-tuple-element.4.src_ref), custom_call_target="tpu_custom_call" | custom-call | bytes 67108864 | tf_op jit(solution)/shard_map/pallas_call | solution.py:236
  536.0 0.0 collective-permute-done.piece_ref
  536.0 1.0 shard_map.52.down_ref
  537.0 18.0 %collective-permute-done.1.piece_ref = bf16[1,512,1024]{2,1,0:T(8,128)(2,1)S(1)} collective-permute-done((bf16[1,512,1024]{2,1,0:T(8,128)(2,1)S(1)}, bf16[1,512,1024]{2,1,0:T(8,128)(2,1)S(1)}, u32[]{:S(2)}, u32[]{:S(2)}) %collective-permute-start.1) | collective-permute-done | bytes 1048608 | tf_op jit(solution)/shard_map/ppermute | solution.py:234
  555.0 1.0 shard_map.53
  556.0 0.7 copy.10
Async XLA Ops:
  506.2 29.8 %collective-permute-start = (bf16[1,512,1024]{2,1,0:T(8,128)(2,1)S(1)}, bf16[1,512,1024]{2,1,0:T(8,128)(2,1)S(1)}, u32[]{:S(2)}, u32[]{:S(2)}) collective-permute-start(bf16[1,512,1024]{2,1,0:T(8,128)(2,1)S(1)} %get-tuple-element.7), channel_id=1, source_target_pairs={{2,3},{1,0},{6,7},{5,4},{10,11},{9,8},{14,15},{13,12},{18,19},{17,... | collective-permute-start | bytes 3145736 | tf_op jit(solution)/shard_map/ppermute | solution.py:234
  507.5 47.5 %collective-permute-start.1 = (bf16[1,512,1024]{2,1,0:T(8,128)(2,1)S(1)}, bf16[1,512,1024]{2,1,0:T(8,128)(2,1)S(1)}, u32[]{:S(2)}, u32[]{:S(2)}) collective-permute-start(bf16[1,512,1024]{2,1,0:T(8,128)(2,1)S(1)} %get-tuple-element.6), channel_id=1, source_target_pairs={{2,3},{1,0},{6,7},{5,4},{10,11},{9,8},{14,15},{13,12},{18,19},{17,... | collective-permute-start | bytes 3145736 | tf_op jit(solution)/shard_map/ppermute | solution.py:234
